TPU v7x, 32 devices: a whole 2x2x4 slice. The times are simulated.
32 devices in a mesh: dp: 4 (over y, x), expert: 8 (over z, core).
Axes of the slice: x: 2, y: 2, z: 4, core: 2. Of those that a mesh axis runs over, the one named last changes fastest.
Arguments:
- shortcut_in: bfloat16 [128, 7168], P('expert', 'dp'), may hold values from -6 to 6
- current_in: bfloat16 [128, 7168], P('expert', 'dp'), may hold values from -6 to 6
- expert_ids: int32 [128, 4], P('expert'), may hold values from 0 to 7, all different within a row; in each aligned block of 16 rows (0 to 15, 16 to 31, ...) at most 12 rows name the same one
- route_weight: float32 [128, 4], P('expert'), may hold values from 0.1 to 1
- gate_weight: bfloat16 [8, 7168, 2048], P('expert', 'dp'), may hold values from -0.09375 to 0.09375
- up_weight: bfloat16 [8, 7168, 2048], P('expert', 'dp'), may hold values from -0.09375 to 0.09375
- down_weight: bfloat16 [8, 2048, 7168], P('expert', None, 'dp'), may hold values from -0.125 to 0.125
- shared_gate: bfloat16 [7168, 2048], P('dp'), may hold values from -0.09375 to 0.09375
- shared_up: bfloat16 [7168, 2048], P('dp'), may hold values from -0.09375 to 0.09375
- shared_down: bfloat16 [2048, 7168], P(None, 'dp'), may hold values from -0.125 to 0.125
Outputs:
- mixed: bfloat16 [128, 7168], P('expert', 'dp')
Inputs may be any that keep to these rules, and one draw needn't show every extreme that they name: `expert_ids`: each row names 4 different experts. In each aligned block of 16 rows (the tokens of one index of the expert axis) no expert is named by more than 12 rows, and in at least one such block some expert is named by exactly 12 rows.
All inputs are finite; a program needn't handle non-finite values.
Results may differ from a plain program's by a relative error of at most 0.035.
Values may be sent and summed in bfloat16 or wider, within the bound.
A program may use at most 128 MiB of HBM per device.

v0:
```python
import jax
import jax.numpy as jnp
from jax import lax
from jax.sharding import PartitionSpec as P


def activate(summed):
    return (jax.nn.silu(summed[:, 0]) * summed[:, 1]).astype(jnp.bfloat16)


def hidden_of(partial_value):
    summed = lax.psum_scatter(
        partial_value.astype(jnp.bfloat16), "dp", scatter_dimension=2, tiled=True
    ).astype(jnp.float32)
    return lax.all_gather(activate(summed), "dp", axis=1, tiled=True)


def send_rows(outgoing):
    return lax.all_to_all(outgoing, "expert", split_axis=0, concat_axis=0, tiled=True)


def expert_partial(arrived, gate_weight, up_weight):
    gate = jnp.einsum("sacd,adh->sach", arrived, gate_weight, preferred_element_type=jnp.float32)
    upper = jnp.einsum("sacd,adh->sach", arrived, up_weight, preferred_element_type=jnp.float32)
    stacked = jnp.stack([gate, upper], axis=3)
    return stacked.reshape(-1, 2, gate_weight.shape[2])


def local(
    shortcut_in,
    current_in,
    expert_ids,
    route_weight,
    gate_weight,
    up_weight,
    down_weight,
    shared_gate,
    shared_up,
    shared_down,
):
    sources = lax.axis_size("expert")
    local_experts = gate_weight.shape[0]
    experts = sources * local_experts
    tokens, top = expert_ids.shape
    capacity = 3 * tokens * top // (2 * experts)
    width = shortcut_in.shape[1]
    hidden_units = gate_weight.shape[2]
    flat_ids = expert_ids.reshape(-1)
    onehot = (flat_ids[:, None] == jnp.arange(experts, dtype=jnp.int32)[None, :]).astype(jnp.int32)
    rank = jnp.sum((jnp.cumsum(onehot, axis=0) - 1) * onehot, axis=1)
    slot = (flat_ids * capacity + rank).reshape(tokens, top)
    positions = jnp.arange(experts * capacity, dtype=jnp.int32)
    place = jnp.sum((slot[None, :, :] == positions[:, None, None]).astype(jnp.bfloat16), axis=2)
    outgoing = jnp.dot(place, shortcut_in, preferred_element_type=jnp.float32).astype(jnp.bfloat16)
    outgoing = outgoing.reshape(sources, local_experts * capacity, width)
    shared_gate_sum = jnp.dot(current_in, shared_gate, preferred_element_type=jnp.float32)
    shared_up_sum = jnp.dot(current_in, shared_up, preferred_element_type=jnp.float32)
    shared_partial = jnp.stack([shared_gate_sum, shared_up_sum], axis=1)
    routed_rows = experts * capacity
    arrived = send_rows(outgoing).reshape(sources, local_experts, capacity, width)
    routed_partial = expert_partial(arrived, gate_weight, up_weight)
    joined = hidden_of(jnp.concatenate([routed_partial, shared_partial], axis=0))
    routed_hidden = joined[:routed_rows]
    shared_hidden = joined[routed_rows:]
    routed_hidden = routed_hidden.reshape(sources, local_experts, capacity, hidden_units)
    expert_out = jnp.einsum(
        "sach,ahd->sacd", routed_hidden, down_weight, preferred_element_type=jnp.float32
    ).astype(jnp.bfloat16)
    returned = lax.all_to_all(
        expert_out.reshape(sources, local_experts * capacity, width),
        "expert",
        split_axis=0,
        concat_axis=0,
        tiled=True,
    )
    picked = returned.reshape(routed_rows, width)[slot]
    routed = jnp.sum(route_weight[:, :, None] * picked.astype(jnp.float32), axis=1)
    shared_out = jnp.dot(shared_hidden, shared_down, preferred_element_type=jnp.float32)
    return (shared_out + routed).astype(jnp.bfloat16)


def solution(mesh):
    placed = (
        P("expert", "dp"),
        P("expert", "dp"),
        P("expert", None),
        P("expert", None),
        P("expert", "dp", None),
        P("expert", "dp", None),
        P("expert", None, "dp"),
        P("dp", None),
        P("dp", None),
        P(None, "dp"),
    )
    return jax.shard_map(
        local, mesh=mesh, in_specs=placed, out_specs=P("expert", "dp"), check_vma=False
    )
```

profile of v0, /device:TPU:0, one launch (start us, length us, event | category | flops | bytes accessed | tf_op | source)
XLA Modules:
  0.0 113.1 jit_solution(13028486477478865265)
XLA Ops:
  6.5 0.8 copy.17
  7.3 0.1 eq.28
  7.5 0.1 reduce_window_sum.11
  7.6 0.2 select_reduce_fusion
  7.7 0.1 reduce_sum.33
  7.9 0.1 copy.19
  7.9 0.1 fusion.29
  8.0 0.3 convolution_convert_fusion
  8.3 0.8 reshape.50
  9.2 6.5 %all-to-all-start = ((bf16[8,12,1792]{2,1,0:T(8,128)(2,1)}), bf16[8,12,1792]{2,1,0:T(8,128)(2,1)S(1)}, u32[]{:S(2)}, u32[]{:S(2)}) async-start(bf16[8,12,1792]{2,1,0:T(8,128)(2,1)} %reshape.50), calls=%async_computation | async-start | bytes 917504 | tf_op jit(solution)/shard_map/all_to_all | solution.py:19
  15.7 4.2 %fusion.22 = bf16[16,1,2048]{2,0,1:T(8,128)(2,1)S(1)} fusion(bf16[16,1792]{1,0:T(8,128)(2,1)} %param.11, bf16[1792,2048]{1,0:T(8,128)(2,1)} %param.17), kind=kOutput, calls=%fused_computation.17 | convolution fusion | flops 117473280 | bytes 7462912 | tf_op jit(solution)/shard_map/dot_general | solution.py:56
  19.9 4.2 %fusion.23 = bf16[16,1,2048]{2,0,1:T(8,128)(2,1)S(1)} fusion(bf16[16,1792]{1,0:T(8,128)(2,1)S(1)} %copy-done.1, bf16[1792,2048]{1,0:T(8,128)(2,1)} %param.18), kind=kOutput, calls=%fused_computation.18 | convolution fusion | flops 117473280 | bytes 7462912 | tf_op jit(solution)/shard_map/dot_general | solution.py:57
  24.1 5.5 %all-to-all-done = bf16[8,12,1792]{2,1,0:T(8,128)(2,1)S(1)} async-done(((bf16[8,12,1792]{2,1,0:T(8,128)(2,1)}), bf16[8,12,1792]{2,1,0:T(8,128)(2,1)S(1)}, u32[]{:S(2)}, u32[]{:S(2)}) %all-to-all-start) | async-done | bytes 344096 | tf_op jit(solution)/shard_map/all_to_all | solution.py:19
  29.6 4.3 %fusion.18 = bf16[8,1,12,2048]{3,2,0,1:T(8,128)(2,1)S(1)} fusion(bf16[8,12,1792]{2,1,0:T(8,128)(2,1)S(1)} %all-to-all-done, bf16[1,1792,2048]{2,1,0:T(8,128)(2,1)} %param.14), kind=kOutput, calls=%fused_computation.12 | convolution fusion | flops 704839680 | bytes 8077312 | tf_op jit(solution)/shard_map/sacd,adh->sach/dot_general | solution.py:23
  33.9 0.1 stack.21
  34.0 4.3 %fusion.15 = bf16[8,1,12,2048]{3,2,0,1:T(8,128)(2,1)S(1)} fusion(bf16[8,12,1792]{2,1,0:T(8,128)(2,1)S(1)} %all-to-all-done, bf16[1,1792,2048]{2,1,0:T(8,128)(2,1)} %param.15), kind=kOutput, calls=%fused_computation.11 | convolution fusion | flops 704839680 | bytes 8077312 | tf_op jit(solution)/shard_map/sacd,adh->sach/dot_general | solution.py:24
  38.3 0.1 stack.22
  38.4 1.0 maximum_maximum_fusion
  39.4 26.2 %reduce-scatter.2.cloned.1.call-done = bf16[112,2,512]{2,0,1:T(8,128)(2,1)} async-done(((bf16[112,2,2048]{2,0,1:T(8,128)(2,1)}), bf16[112,2,512]{2,0,1:T(8,128)(2,1)}) %reduce-scatter.2.cloned.1.call-update) | async-done | bytes 229392 | tf_op jit(solution)/shard_map/reduce_scatter | solution.py:12
  65.6 1.0 convert_element_type.33
  66.7 9.8 %all_gather.3 = bf16[112,2048]{1,0:T(8,128)(2,1)S(1)} all-gather(bf16[112,512]{1,0:T(8,128)(2,1)S(1)} %fusion.25), channel_id=1, replica_groups=mesh['dp'=4,'expert'=8] {'dp'}, dimensions={1}, use_global_device_ids=true | all-gather | bytes 573440 | tf_op jit(solution)/shard_map/all_gather | solution.py:15
  76.5 0.1 reshape.53
  76.6 5.0 %fusion.12 = bf16[8,12,1792]{2,1,0:T(8,128)(2,1)} fusion(bf16[8,12,2048]{2,1,0:T(8,128)(2,1)S(1)} %reshape.53, bf16[1,2048,1792]{2,1,0:T(8,128)(2,1)} %param.16), kind=kOutput, calls=%fused_computation.9 | convolution fusion | flops 704815104 | bytes 8077312 | tf_op jit(solution)/shard_map/sach,ahd->sacd/dot_general | solution.py:66
  81.6 4.6 %all-to-all-start.1 = ((bf16[8,12,1792]{2,1,0:T(8,128)(2,1)}), bf16[8,12,1792]{2,1,0:T(8,128)(2,1)S(1)}, u32[]{:S(2)}, u32[]{:S(2)}) async-start(bf16[8,12,1792]{2,1,0:T(8,128)(2,1)} %fusion.12), calls=%async_computation.2 | async-start | bytes 917504 | tf_op jit(solution)/shard_map/all_to_all | solution.py:69
  86.2 0.1 reshape.58
  86.3 0.1 copy.20
  86.4 13.7 %all-to-all-done.1 = bf16[8,12,1792]{2,1,0:T(8,128)(2,1)S(1)} async-done(((bf16[8,12,1792]{2,1,0:T(8,128)(2,1)}), bf16[8,12,1792]{2,1,0:T(8,128)(2,1)S(1)}, u32[]{:S(2)}, u32[]{:S(2)}) %all-to-all-start.1) | async-done | bytes 344096 | tf_op jit(solution)/shard_map/all_to_all | solution.py:69
  100.2 0.1 reshape.55
  100.2 0.7 gather_fusion
  101.0 0.1 reshape.66
  101.1 0.3 multiply_reduce_fusion
  101.5 4.8 %fusion.21 = bf16[16,1792]{1,0:T(8,128)(2,1)} fusion(f32[16,1792]{1,0:T(8,128)S(1)} %multiply_reduce_fusion, bf16[2048,1792]{1,0:T(8,128)(2,1)} %param.19, bf16[112,2048]{1,0:T(8,128)(2,1)S(1)} %all_gather.3), kind=kOutput, calls=%fused_computation.14 | convolution fusion | flops 117497856 | bytes 7577600 | tf_op jit(solution)/shard_map/dot_general | solution.py:78
  (13 shorter events, 0.3 us)
Async XLA Ops:
  6.5 1.5 %copy-start = (bf16[16,1792]{1,0:T(8,128)(2,1)S(1)}, bf16[16,1792]{1,0:T(8,128)(2,1)}, u32[]{:S(2)}) copy-start(bf16[16,1792]{1,0:T(8,128)(2,1)} %param.10) | copy-start | bytes 172036
  9.2 10.7 %copy-start.1 = (bf16[16,1792]{1,0:T(8,128)(2,1)S(1)}, bf16[16,1792]{1,0:T(8,128)(2,1)}, u32[]{:S(2)}) copy-start(bf16[16,1792]{1,0:T(8,128)(2,1)} %param.11) | copy-start | bytes 172036
  9.2 20.4 %all-to-all-start = ((bf16[8,12,1792]{2,1,0:T(8,128)(2,1)}), bf16[8,12,1792]{2,1,0:T(8,128)(2,1)S(1)}, u32[]{:S(2)}, u32[]{:S(2)}) async-start(bf16[8,12,1792]{2,1,0:T(8,128)(2,1)} %reshape.50), calls=%async_computation | async-start | bytes 917504 | tf_op jit(solution)/shard_map/all_to_all | solution.py:19
  15.7 49.9 %reduce-scatter.2.cloned.1.call-start = ((), (), s32[]{:S(2)}) async-start(), calls=%async_computation.3 | async-start | bytes 1146880 | tf_op jit(solution)/shard_map/reduce_scatter | solution.py:12
  66.6 19.7 %copy-start.2 = (f32[16,4]{0,1:T(4,128)S(1)}, f32[16,4]{0,1:T(4,128)}, u32[]{:S(2)}) copy-start(f32[16,4]{0,1:T(4,128)} %param.13) | copy-start | bytes 772
  81.6 18.5 %all-to-all-start.1 = ((bf16[8,12,1792]{2,1,0:T(8,128)(2,1)}), bf16[8,12,1792]{2,1,0:T(8,128)(2,1)S(1)}, u32[]{:S(2)}, u32[]{:S(2)}) async-start(bf16[8,12,1792]{2,1,0:T(8,128)(2,1)} %fusion.12), calls=%async_computation.2 | async-start | bytes 917504 | tf_op jit(solution)/shard_map/all_to_all | solution.py:69
Sparse Core Ops, SparseCore 0:
  39.6 25.9 reduce-scatter.1
where the time goes:
time: 114 us; the launch traced here: 113 us
  waiting for transfers between devices  45.5 us (40%)
  matrix products  27 us (24%)
  between operations  13.5 us (12%)
  starting transfers between devices  11.1 us (10%)
  blocking collectives  9.81 us (9%)
  local copies, waits for them, and re-layouts  3.27 us (3%)
  other arithmetic  2.85 us (2%)
    reduce_scatter x1, waiting for transfers between devices, hidden_of(): lax.psum_scatter(partial_value.astype(jnp.bfloat16), 'dp', scatter_dimens...  26.2 us
    all_to_all x1, waiting for transfers between devices, local(): lax.all_to_all(expert_out.reshape(sources, local_experts * capacity, widt...  13.7 us
    all_gather x1, blocking collectives, hidden_of(): return lax.all_gather(activate(summed), 'dp', axis=1, tiled=True)  9.81 us
    all_to_all x1, starting transfers between devices, send_rows(): lax.all_to_all(outgoing, 'expert', split_axis=0, concat_axis=0, tiled=True)  6.49 us
    all_to_all x1, waiting for transfers between devices, send_rows(): lax.all_to_all(outgoing, 'expert', split_axis=0, concat_axis=0, tiled=True)  5.53 us
    dot_general x1, matrix products, local(): jnp.einsum('sach,ahd->sacd', routed_hidden, down_weight, preferred_elemen...  5.01 us
    dot_general x1, matrix products, local(): jnp.dot(shared_hidden, shared_down, preferred_element_type=jnp.float32)  4.78 us
    all_to_all x1, starting transfers between devices, local(): lax.all_to_all(expert_out.reshape(sources, local_experts * capacity, widt...  4.61 us
  transfers between devices with their start and end apart: 3, of which 3 were waited for; matrix products, arithmetic and copies ran while one was open for 8% of the time, Pallas kernels for 0%

commit v1 on v0

--- a/solution.py
+++ b/solution.py
@@ -1,6 +1,10 @@
+import functools
+
 import jax
 import jax.numpy as jnp
 from jax import lax
+from jax.experimental import pallas as pl
+from jax.experimental.pallas import tpu as pltpu
 from jax.sharding import PartitionSpec as P
 
 
@@ -79,6 +83,270 @@
     return (shared_out + routed).astype(jnp.bfloat16)
 
 
+MESH = pl.DeviceIdType.MESH
+BF = jnp.bfloat16
+F32 = jnp.float32
+PARTS = 2
+
+
+def dot(a, b):
+    return jnp.dot(a, b, preferred_element_type=F32)
+
+
+def layer_kernel(
+    n_dp, n_e, rows,
+    x_ref, cur_ref, ids_ref, w_ref, gate_hbm, up_hbm, down_hbm, sg_hbm, su_hbm, sd_hbm,
+    out_ref,
+    gate_v, up_v, down_v, sg_v, su_v, sd_v,
+    m_own, m_all, x_all, c_all, xc, part, rs_in, hid, acc,
+    sh_part, sh_in, sh_hid, contrib, pair_in, fin_out, fin_in,
+    gate_sem, up_sem, down_sem, shw_sem,
+    m_s, m_r, x_s, x_r, c_s, c_r, mp_s, mp_r, xp_s, xp_r, cp_s, cp_r,
+    rs_s, rs_r, hid_s, hid_r, shp_s, shp_r, shh_s, shh_r, pair_s, pair_r, fin_s, fin_r,
+):
+    me_d = lax.axis_index("dp")
+    me_e = lax.axis_index("expert")
+    zs = n_e // 2
+    z, c = me_e // 2, lax.rem(me_e, 2)
+    partner = 2 * z + (1 - c)
+    tokens, width = x_ref.shape
+    chunk = gate_v.shape[2]
+    hs = chunk * PARTS
+    total = n_e * tokens
+    sh = sg_v.shape[1]
+    share = total // n_dp
+    slots = [(q, s) for q in range(PARTS) for s in [*range(1, n_dp), 0]]
+
+    def start(copy):
+        copy.start()
+        return copy
+
+    def dp_dev(s):
+        return lax.rem(me_d + s, n_dp)
+
+    def dp_src(s):
+        return lax.rem(me_d - s + n_dp, n_dp)
+
+    def z_dev(s):
+        return 2 * lax.rem(z + s, zs) + c
+
+    def z_src(s):
+        return 2 * lax.rem(z - s + zs, zs) + c
+
+    local_waits = {}
+    for i, (q, s) in enumerate(slots):
+        col = pl.ds(pl.multiple_of(dp_dev(s) * hs + q * chunk, 128), chunk)
+        local_waits["g", q, s] = start(pltpu.make_async_copy(gate_hbm.at[0, :, col], gate_v.at[i], gate_sem.at[i]))
+        local_waits["u", q, s] = start(pltpu.make_async_copy(up_hbm.at[0, :, col], up_v.at[i], up_sem.at[i]))
+    own = pl.ds(pl.multiple_of(me_e * sh, 128), sh)
+    local_waits["sg"] = start(pltpu.make_async_copy(sg_hbm.at[:, own], sg_v, shw_sem.at[0]))
+    local_waits["su"] = start(pltpu.make_async_copy(su_hbm.at[:, own], su_v, shw_sem.at[1]))
+    local_waits["sd"] = start(pltpu.make_async_copy(sd_hbm.at[own, :], sd_v, shw_sem.at[2]))
+    for i, (q, s) in enumerate(slots):
+        row = pl.ds(pl.multiple_of(dp_src(s) * hs + q * chunk, 128), chunk)
+        local_waits["d", q, s] = start(pltpu.make_async_copy(down_hbm.at[0, row, :], down_v.at[i], down_sem.at[i]))
+
+    barrier = pltpu.get_barrier_semaphore()
+    for s in range(1, n_dp):
+        pl.semaphore_signal(barrier, inc=1, device_id=(dp_dev(s), me_e), device_id_type=MESH)
+    for s in range(1, zs):
+        pl.semaphore_signal(barrier, inc=1, device_id=(me_d, z_dev(s)), device_id_type=MESH)
+    pl.semaphore_signal(barrier, inc=1, device_id=(me_d, partner), device_id_type=MESH)
+
+    lanes = lax.broadcasted_iota(jnp.int32, (tokens, 128), 1)
+    ids, weight = ids_ref[...], w_ref[...]
+    mine = jnp.zeros((tokens, 128), F32)
+    for k in range(ids.shape[1]):
+        mine += jnp.where(ids[:, k:k + 1] == lanes, weight[:, k:k + 1], 0.0)
+    m_own[...] = mine
+    m_all[me_e] = mine
+    x_all[me_e] = x_ref[...]
+    c_all[me_e] = cur_ref[...]
+    pl.semaphore_wait(barrier, n_dp - 1 + zs - 1 + 1)
+
+    sends = []
+
+    def remote(src, dst, ssem, rsem, dp, e):
+        copy = pltpu.make_async_remote_copy(
+            src_ref=src, dst_ref=dst, send_sem=ssem, recv_sem=rsem, device_id=(dp, e), device_id_type=MESH
+        )
+        copy.start()
+        sends.append(copy)
+
+    def arrived(dst, ssem, rsem):
+        pltpu.make_async_remote_copy(
+            src_ref=dst, dst_ref=dst, send_sem=ssem, recv_sem=rsem, device_id=(me_d, partner), device_id_type=MESH
+        ).wait_recv()
+
+    groups = [(m_own, m_all, m_s, m_r, mp_s, mp_r), (x_ref, x_all, x_s, x_r, xp_s, xp_r), (cur_ref, c_all, c_s, c_r, cp_s, cp_r)]
+
+    def spread(src, buf, ss, rr, ps, pr):
+        for s in range(zs - 1, 0, -1):
+            remote(src, buf.at[me_e], ss.at[s], rr.at[s], me_d, z_dev(s))
+        remote(src, buf.at[me_e], ps.at[0], pr.at[0], me_d, partner)
+
+    def relay(src, buf, ss, rr, ps, pr):
+        for s in range(1, zs):
+            block = buf.at[z_src(s)]
+            arrived(block, ss.at[s], rr.at[s])
+            remote(block, block, ps.at[s], pr.at[s], me_d, partner)
+
+    def collect(src, buf, ss, rr, ps, pr):
+        for s in range(zs):
+            arrived(buf.at[z_src(s) + 1 - 2 * c], ps.at[s], pr.at[s])
+
+    spread(*groups[0])
+    spread(*groups[1])
+    relay(*groups[0])
+    collect(*groups[0])
+    routing = m_all[...].reshape(total, 128)
+    named = jnp.where(routing > 0, 1.0, 0.0)
+    below = lax.broadcasted_iota(jnp.int32, (total, total), 1) < lax.broadcasted_iota(jnp.int32, (total, total), 0)
+    rank = dot(jnp.where(below, 1.0, 0.0).astype(BF), named.astype(BF))
+    pick = lax.broadcasted_iota(jnp.int32, (total, 128), 1) == me_e
+    rank_col = jnp.sum(jnp.where(pick, rank, 0.0), axis=1, keepdims=True)
+    scale_col = jnp.sum(jnp.where(pick, routing, 0.0), axis=1, keepdims=True)
+    padded = -(-rows // 128) * 128
+    slot = lax.broadcasted_iota(jnp.int32, (total, padded), 1).astype(F32)
+    placed_t = jnp.where(jnp.logical_and(slot == rank_col, scale_col > 0), 1.0, 0.0)
+    gather = jnp.transpose(placed_t)[:rows].astype(BF)
+    scatter = placed_t.astype(BF)[:, :rows]
+
+    relay(*groups[1])
+    spread(*groups[2])
+    collect(*groups[1])
+    xc[...] = dot(gather, x_all[...].reshape(total, width)).astype(BF)
+
+    for i, (q, s) in enumerate(slots):
+        local_waits["g", q, s].wait()
+        local_waits["u", q, s].wait()
+        part[i, :, :chunk] = dot(xc[...], gate_v[i]).astype(BF)
+        part[i, :, chunk:] = dot(xc[...], up_v[i]).astype(BF)
+        if s:
+            remote(part.at[i], rs_in.at[i], rs_s.at[i], rs_r.at[i], dp_dev(s), me_e)
+
+    relay(*groups[2])
+    collect(*groups[2])
+    local_waits["sg"].wait()
+    local_waits["su"].wait()
+    cur = c_all[...].reshape(total, width)
+    sh_part[:, :, :sh] = dot(cur, sg_v[...]).astype(BF).reshape(n_dp, share, sh)
+    sh_part[:, :, sh:] = dot(cur, su_v[...]).astype(BF).reshape(n_dp, share, sh)
+    for s in range(1, n_dp):
+        remote(sh_part.at[dp_dev(s)], sh_in.at[s], shp_s.at[s], shp_r.at[s], dp_dev(s), me_e)
+
+    def act(term, n):
+        gate, upper = term[:, :n], term[:, n:]
+        return (gate / (1.0 + jnp.exp(-gate)) * upper).astype(BF)
+
+    def routed_act(q):
+        base = q * n_dp
+        term = part[base + n_dp - 1].astype(F32)
+        for s in range(1, n_dp):
+            i = base + s - 1
+            arrived(rs_in.at[i], rs_s.at[i], rs_r.at[i])
+            term = term + rs_in[i].astype(F32)
+        j = base + n_dp - 1
+        hid[j] = act(term, chunk)
+        for s in range(1, n_dp):
+            i = base + s - 1
+            remote(hid.at[j], hid.at[i], hid_s.at[i], hid_r.at[i], dp_dev(s), me_e)
+
+    def routed_down(q, first):
+        base = q * n_dp
+        for s in [0, *range(1, n_dp)]:
+            i = base + (s - 1 if s else n_dp - 1)
+            if s:
+                arrived(hid.at[i], hid_s.at[i], hid_r.at[i])
+            local_waits["d", q, s].wait()
+            value = dot(hid[i], down_v[i])
+            acc[...] = value if first and s == 0 else acc[...] + value
+
+    for q in range(PARTS):
+        routed_act(q)
+    term = sh_part[me_d].astype(F32)
+    for s in range(1, n_dp):
+        arrived(sh_in.at[s], shp_s.at[s], shp_r.at[s])
+        term = term + sh_in[s].astype(F32)
+    sh_hid[me_d] = act(term, sh)
+    for s in range(1, n_dp):
+        remote(sh_hid.at[me_d], sh_hid.at[me_d], shh_s.at[s], shh_r.at[s], dp_dev(s), me_e)
+    for q in range(PARTS):
+        routed_down(q, q == 0)
+    for s in range(1, n_dp):
+        arrived(sh_hid.at[dp_src(s)], shh_s.at[s], shh_r.at[s])
+    local_waits["sd"].wait()
+    value = dot(sh_hid[...].reshape(total, sh), sd_v[...])
+    value = value + scale_col * dot(scatter, acc[...].astype(BF))
+    contrib[...] = value.astype(BF).reshape(n_e, tokens, width)
+    order = [*range(zs - 1, -1, -1)]
+    for s in order:
+        remote(contrib.at[2 * lax.rem(z + s, zs) + 1 - c], pair_in.at[s], pair_s.at[s], pair_r.at[s], me_d, partner)
+    for s in order:
+        arrived(pair_in.at[s], pair_s.at[s], pair_r.at[s])
+        both = contrib[z_dev(s)].astype(F32) + pair_in[s].astype(F32)
+        if s:
+            fin_out[s] = both.astype(BF)
+            remote(fin_out.at[s], fin_in.at[s], fin_s.at[s], fin_r.at[s], me_d, z_dev(s))
+    for s in range(1, zs):
+        arrived(fin_in.at[s], fin_s.at[s], fin_r.at[s])
+        both = both + fin_in[s].astype(F32)
+    out_ref[...] = both.astype(BF)
+    for copy in sends:
+        copy.wait_send()
+
+
+def fused(n_dp, n_e, shortcut_in, current_in, expert_ids, route_weight, gate_weight, up_weight, down_weight, shared_gate, shared_up, shared_down):
+    tokens, width = shortcut_in.shape
+    hidden = gate_weight.shape[2]
+    top = expert_ids.shape[1]
+    capacity = 3 * tokens * top // (2 * n_e)
+    rows = min(-(-capacity * n_e // 16) * 16, n_e * tokens)
+    chunk = hidden // n_dp // PARTS
+    count = PARTS * n_dp
+    sh = hidden // n_e
+    zs = n_e // 2
+    total = n_e * tokens
+    share = total // n_dp
+    V = pltpu.VMEM
+    S = pltpu.SemaphoreType.DMA
+    scratch = [
+        V((count, width, chunk), BF), V((count, width, chunk), BF), V((count, chunk, width), BF),
+        V((width, sh), BF), V((width, sh), BF), V((sh, width), BF),
+        V((tokens, 128), F32), V((n_e, tokens, 128), F32), V((n_e, tokens, width), BF), V((n_e, tokens, width), BF),
+        V((rows, width), BF), V((count, rows, 2 * chunk), BF), V((count, rows, 2 * chunk), BF),
+        V((count, rows, chunk), BF), V((rows, width), F32),
+        V((n_dp, share, 2 * sh), BF), V((n_dp, share, 2 * sh), BF), V((n_dp, share, sh), BF),
+        V((n_e, tokens, width), BF), V((zs, tokens, width), BF), V((zs, tokens, width), BF), V((zs, tokens, width), BF),
+        S((count,)), S((count,)), S((count,)), S((3,)),
+        *[S((zs,)) for _ in range(12)],
+        *[S((count,)) for _ in range(4)],
+        *[S((n_dp,)) for _ in range(4)],
+        *[S((zs,)) for _ in range(4)],
+    ]
+    vm = pl.BlockSpec(memory_space=pltpu.VMEM)
+    hbm = pl.BlockSpec(memory_space=pl.ANY)
+    return pl.pallas_call(
+        functools.partial(layer_kernel, n_dp, n_e, rows),
+        out_shape=jax.ShapeDtypeStruct((tokens, width), BF),
+        in_specs=[vm] * 4 + [hbm] * 6,
+        out_specs=vm,
+        scratch_shapes=scratch,
+        compiler_params=pltpu.CompilerParams(collective_id=0, has_side_effects=True, vmem_limit_bytes=60 * 1024 * 1024),
+    )(shortcut_in, current_in, expert_ids, route_weight, gate_weight, up_weight, down_weight, shared_gate, shared_up, shared_down)
+
+
+def body(n_dp, n_e, *arrays):
+    tokens, width = arrays[0].shape
+    experts, _, hidden = arrays[4].shape
+    aligned = (
+        experts == 1 and n_e % 2 == 0 and n_e <= 128 and tokens % 16 == 0 and width % 128 == 0
+        and hidden % (n_dp * PARTS * 128) == 0 and hidden % (n_e * 128) == 0
+        and n_e * tokens % (n_dp * 16) == 0
+    )
+    return fused(n_dp, n_e, *arrays) if aligned else local(*arrays)
+
+
 def solution(mesh):
     placed = (
         P("expert", "dp"),
@@ -93,5 +361,5 @@
         P(None, "dp"),
     )
     return jax.shard_map(
-        local, mesh=mesh, in_specs=placed, out_specs=P("expert", "dp"), check_vma=False
+        functools.partial(body, mesh.shape["dp"], mesh.shape["expert"]), mesh=mesh, in_specs=placed, out_specs=P("expert", "dp"), check_vma=False
     )

time: 114 us -> 46.5 us (0.41)
  waiting for transfers between devices: 45.5 us -> 0 us
  Pallas kernels: 0 us -> 42.1 us
  matrix products: 27 us -> 0 us
  between operations: 13.5 us -> 0.01 us
  starting transfers between devices: 11.1 us -> 0 us
  blocking collectives: 9.81 us -> 0 us
  other arithmetic: 2.85 us -> 0 us
    pallas_call x0 -> x1, Pallas kernels: none -> 42.1 us  [fused(): pl.pallas_call(functools.partial(layer_kernel, n_dp, n_e, rows), out_shap...]
    dot_general x7 -> x0, matrix products: 27 us -> none  [the longest x1 5.01 us: local(): jnp.einsum('sach,ahd->sacd', routed_hidden, down_weight, preferred_elemen...]
    reduce_scatter x1 -> x0, waiting for transfers between devices: 26.2 us -> none  [hidden_of(): lax.psum_scatter(partial_value.astype(jnp.bfloat16), 'dp', scatter_dimens...]
    all_to_all x2 -> x0, waiting for transfers between devices: 19.3 us -> none  [the longest x1 13.7 us: local(): lax.all_to_all(expert_out.reshape(sources, local_experts * capacity, widt...]
    all_to_all x2 -> x0, starting transfers between devices: 11.1 us -> none  [the longest x1 6.49 us: send_rows(): lax.all_to_all(outgoing, 'expert', split_axis=0, concat_axis=0, tiled=True)]
    all_gather x1 -> x0, blocking collectives: 9.81 us -> none  [hidden_of(): return lax.all_gather(activate(summed), 'dp', axis=1, tiled=True)]
    unnamed x8 -> x3, local copies, waits for them, and re-layouts: 0.86 us -> 4.15 us
  transfers between devices with their start and end apart: 3 -> 0, of which waited for: 3 -> 0; matrix products, arithmetic and copies ran while one was open for 8% -> 0% of each run, Pallas kernels for 0% -> 0%
where the time goes in v1:
time: 46.5 us; the launch traced here: 46.2 us
  Pallas kernels  42.1 us (91%)
  local copies, waits for them, and re-layouts  4.15 us (9%)
    pallas_call x1, Pallas kernels, fused(): pl.pallas_call(functools.partial(layer_kernel, n_dp, n_e, rows), out_shap...  42.1 us
    unnamed x3, local copies, waits for them, and re-layouts  4.15 us

profile of v1, /device:TPU:0, one launch (start us, length us, event | category | flops | bytes accessed | tf_op | source)
XLA Modules:
  0.0 46.2 jit_solution(6853152523956084935)
XLA Ops:
  0.0 1.4 %copy.11.ids_ref = s32[16,4]{1,0:T(8,128)} copy(s32[16,4]{0,1:T(4,128)} %param.12) | data formatting | bytes 512 | tf_op args[2]
  1.4 1.3 %copy.12.w_ref = f32[16,4]{1,0:T(8,128)} copy(f32[16,4]{0,1:T(4,128)} %param.13) | data formatting | bytes 512 | tf_op args[3]
  2.7 42.1 %shard_map.100 = bf16[16,1792]{1,0:T(8,128)(2,1)} custom-call(bf16[16,1792]{1,0:T(8,128)(2,1)} %x_ref.1, bf16[16,1792]{1,0:T(8,128)(2,1)} %cur_ref.1, s32[16,4]{1,0:T(8,128)} %copy.11.ids_ref, f32[16,4]{1,0:T(8,128)} %copy.12.w_ref, bf16[1,1792,2048]{2,1,0:T(8,128)(2,1)} %gate_hbm.1, bf16[1,1792,2048]{2,1,0:T(8,128)(2,1)} %up_hbm.1, ...), custom_call_target="tpu_custom_call" | custom-call | tf_op jit(solution)/shard_map/pallas_call | solution.py:329
  44.8 1.4 %copy.14 = bf16[16,1792]{1,0:T(8,128)(2,1)} copy(bf16[16,1792]{1,0:T(8,128)(2,1)} %shard_map.100) | data formatting | bytes 114688

commit v2 on v1

--- a/solution.py
+++ b/solution.py
@@ -98,8 +98,8 @@
     x_ref, cur_ref, ids_ref, w_ref, gate_hbm, up_hbm, down_hbm, sg_hbm, su_hbm, sd_hbm,
     out_ref,
     gate_v, up_v, down_v, sg_v, su_v, sd_v,
-    m_own, m_all, x_all, c_all, xc, part, rs_in, hid, acc,
-    sh_part, sh_in, sh_hid, contrib, pair_in, fin_out, fin_in,
+    flip, m_own, m_all, x_all, c_all, xc, part, rs_in, hid, acc, shv,
+    sh_part, sh_in, sh_hid, own_sum, contrib, pair_in, fin_out, fin_in,
     gate_sem, up_sem, down_sem, shw_sem,
     m_s, m_r, x_s, x_r, c_s, c_r, mp_s, mp_r, xp_s, xp_r, cp_s, cp_r,
     rs_s, rs_r, hid_s, hid_r, shp_s, shp_r, shh_s, shh_r, pair_s, pair_r, fin_s, fin_r,
@@ -108,6 +108,8 @@
     me_e = lax.axis_index("expert")
     zs = n_e // 2
     z, c = me_e // 2, lax.rem(me_e, 2)
+    pairs = zs // 2
+    p, b = z // 2, lax.rem(z, 2)
     partner = 2 * z + (1 - c)
     tokens, width = x_ref.shape
     chunk = gate_v.shape[2]
@@ -128,10 +130,13 @@
         return lax.rem(me_d - s + n_dp, n_dp)
 
     def z_dev(s):
-        return 2 * lax.rem(z + s, zs) + c
+        return 2 * (2 * lax.rem(p + s // 2, pairs) + lax.rem(b + s % 2, 2)) + c
 
     def z_src(s):
-        return 2 * lax.rem(z - s + zs, zs) + c
+        return 2 * (2 * lax.rem(p - s // 2 + pairs, pairs) + lax.rem(b + s % 2, 2)) + c
+
+    def group_blocks(a):
+        return pl.ds(4 * lax.rem(p - a + pairs, pairs), 4)
 
     local_waits = {}
     for i, (q, s) in enumerate(slots):
@@ -153,11 +158,15 @@
         pl.semaphore_signal(barrier, inc=1, device_id=(me_d, z_dev(s)), device_id_type=MESH)
     pl.semaphore_signal(barrier, inc=1, device_id=(me_d, partner), device_id_type=MESH)
 
-    lanes = lax.broadcasted_iota(jnp.int32, (tokens, 128), 1)
-    ids, weight = ids_ref[...], w_ref[...]
-    mine = jnp.zeros((tokens, 128), F32)
-    for k in range(ids.shape[1]):
-        mine += jnp.where(ids[:, k:k + 1] == lanes, weight[:, k:k + 1], 0.0)
+    top = ids_ref.shape[0]
+    flip[...] = jnp.zeros_like(flip)
+    flip[:top, :tokens] = ids_ref[...].astype(F32)
+    flip[top:2 * top, :tokens] = w_ref[...]
+    named_ids = lax.broadcasted_iota(jnp.int32, (128, 128), 0).astype(F32)
+    table = jnp.zeros((128, 128), F32)
+    for k in range(top):
+        table += jnp.where(flip[k:k + 1, :] == named_ids, flip[top + k:top + k + 1, :], 0.0)
+    mine = jnp.transpose(table)[:tokens]
     m_own[...] = mine
     m_all[me_e] = mine
     x_all[me_e] = x_ref[...]
@@ -181,66 +190,62 @@
     groups = [(m_own, m_all, m_s, m_r, mp_s, mp_r), (x_ref, x_all, x_s, x_r, xp_s, xp_r), (cur_ref, c_all, c_s, c_r, cp_s, cp_r)]
 
     def spread(src, buf, ss, rr, ps, pr):
-        for s in range(zs - 1, 0, -1):
+        remote(src, buf.at[me_e], ps.at[0], pr.at[0], me_d, partner)
+        for s in range(1, zs):
             remote(src, buf.at[me_e], ss.at[s], rr.at[s], me_d, z_dev(s))
-        remote(src, buf.at[me_e], ps.at[0], pr.at[0], me_d, partner)
-
-    def relay(src, buf, ss, rr, ps, pr):
-        for s in range(1, zs):
+
+    def relay(s, src, buf, ss, rr, ps, pr):
+        if s:
             block = buf.at[z_src(s)]
             arrived(block, ss.at[s], rr.at[s])
             remote(block, block, ps.at[s], pr.at[s], me_d, partner)
 
-    def collect(src, buf, ss, rr, ps, pr):
-        for s in range(zs):
-            arrived(buf.at[z_src(s) + 1 - 2 * c], ps.at[s], pr.at[s])
+    def collect(s, src, buf, ss, rr, ps, pr):
+        arrived(buf.at[z_src(s) + 1 - 2 * c], ps.at[s], pr.at[s])
 
     spread(*groups[0])
     spread(*groups[1])
-    relay(*groups[0])
-    collect(*groups[0])
-    routing = m_all[...].reshape(total, 128)
-    named = jnp.where(routing > 0, 1.0, 0.0)
-    below = lax.broadcasted_iota(jnp.int32, (total, total), 1) < lax.broadcasted_iota(jnp.int32, (total, total), 0)
-    rank = dot(jnp.where(below, 1.0, 0.0).astype(BF), named.astype(BF))
-    pick = lax.broadcasted_iota(jnp.int32, (total, 128), 1) == me_e
-    rank_col = jnp.sum(jnp.where(pick, rank, 0.0), axis=1, keepdims=True)
-    scale_col = jnp.sum(jnp.where(pick, routing, 0.0), axis=1, keepdims=True)
+    spread(*groups[2])
+    held = 4 * tokens
+    below = lax.broadcasted_iota(jnp.int32, (held, held), 1) < lax.broadcasted_iota(jnp.int32, (held, held), 0)
+    below = jnp.where(below, 1.0, 0.0).astype(BF)
+    pick = lax.broadcasted_iota(jnp.int32, (held, 128), 1) == me_e
     padded = -(-rows // 128) * 128
-    slot = lax.broadcasted_iota(jnp.int32, (total, padded), 1).astype(F32)
-    placed_t = jnp.where(jnp.logical_and(slot == rank_col, scale_col > 0), 1.0, 0.0)
-    gather = jnp.transpose(placed_t)[:rows].astype(BF)
-    scatter = placed_t.astype(BF)[:, :rows]
-
-    relay(*groups[1])
-    spread(*groups[2])
-    collect(*groups[1])
-    xc[...] = dot(gather, x_all[...].reshape(total, width)).astype(BF)
-
-    for i, (q, s) in enumerate(slots):
-        local_waits["g", q, s].wait()
-        local_waits["u", q, s].wait()
-        part[i, :, :chunk] = dot(xc[...], gate_v[i]).astype(BF)
-        part[i, :, chunk:] = dot(xc[...], up_v[i]).astype(BF)
-        if s:
-            remote(part.at[i], rs_in.at[i], rs_s.at[i], rs_r.at[i], dp_dev(s), me_e)
-
-    relay(*groups[2])
-    collect(*groups[2])
-    local_waits["sg"].wait()
-    local_waits["su"].wait()
-    cur = c_all[...].reshape(total, width)
-    sh_part[:, :, :sh] = dot(cur, sg_v[...]).astype(BF).reshape(n_dp, share, sh)
-    sh_part[:, :, sh:] = dot(cur, su_v[...]).astype(BF).reshape(n_dp, share, sh)
-    for s in range(1, n_dp):
-        remote(sh_part.at[dp_dev(s)], sh_in.at[s], shp_s.at[s], shp_r.at[s], dp_dev(s), me_e)
+    slot = lax.broadcasted_iota(jnp.int32, (held, padded), 1).astype(F32)
+    combine = []
+    for a in range(pairs):
+        for s in (2 * a, 2 * a + 1):
+            relay(s, *groups[0])
+        for s in (2 * a, 2 * a + 1):
+            relay(s, *groups[1])
+        for s in (2 * a, 2 * a + 1):
+            collect(s, *groups[0])
+        routing = m_all[group_blocks(a)].reshape(held, 128)
+        rank = dot(below, jnp.where(routing > 0, 1.0, 0.0).astype(BF))
+        rank_col = jnp.sum(jnp.where(pick, rank, 0.0), axis=1, keepdims=True)
+        scale_col = jnp.sum(jnp.where(pick, routing, 0.0), axis=1, keepdims=True)
+        placed_t = jnp.where(jnp.logical_and(slot == rank_col, scale_col > 0), 1.0, 0.0)
+        gather = jnp.transpose(placed_t)[:rows].astype(BF)
+        combine.append((placed_t.astype(BF)[:, :rows], scale_col))
+        for s in (2 * a, 2 * a + 1):
+            collect(s, *groups[1])
+        xc[a] = dot(gather, x_all[group_blocks(a)].reshape(held, width)).astype(BF)
+        for i, (q, s) in enumerate(slots):
+            if a == 0:
+                local_waits["g", q, s].wait()
+                local_waits["u", q, s].wait()
+            n = a * len(slots) + i
+            part[n, :, :chunk] = dot(xc[a], gate_v[i]).astype(BF)
+            part[n, :, chunk:] = dot(xc[a], up_v[i]).astype(BF)
+            if s:
+                remote(part.at[n], rs_in.at[n], rs_s.at[n], rs_r.at[n], dp_dev(s), me_e)
 
     def act(term, n):
         gate, upper = term[:, :n], term[:, n:]
         return (gate / (1.0 + jnp.exp(-gate)) * upper).astype(BF)
 
-    def routed_act(q):
-        base = q * n_dp
+    def routed_act(a, q):
+        base = a * len(slots) + q * n_dp
         term = part[base + n_dp - 1].astype(F32)
         for s in range(1, n_dp):
             i = base + s - 1
@@ -252,18 +257,32 @@
             i = base + s - 1
             remote(hid.at[j], hid.at[i], hid_s.at[i], hid_r.at[i], dp_dev(s), me_e)
 
-    def routed_down(q, first):
-        base = q * n_dp
-        for s in [0, *range(1, n_dp)]:
-            i = base + (s - 1 if s else n_dp - 1)
-            if s:
-                arrived(hid.at[i], hid_s.at[i], hid_r.at[i])
-            local_waits["d", q, s].wait()
-            value = dot(hid[i], down_v[i])
-            acc[...] = value if first and s == 0 else acc[...] + value
-
+    def routed_down(a):
+        for q in range(PARTS):
+            base = q * n_dp
+            for s in [0, *range(1, n_dp)]:
+                i = base + (s - 1 if s else n_dp - 1)
+                n = a * len(slots) + i
+                if s:
+                    arrived(hid.at[n], hid_s.at[n], hid_r.at[n])
+                if a == pairs - 1:
+                    local_waits["d", q, s].wait()
+                value = dot(hid[n], down_v[i])
+                acc[...] = value if q == 0 and s == 0 else acc[...] + value
+
+    for s in range(1, zs):
+        relay(s, *groups[2])
+    for s in range(zs):
+        collect(s, *groups[2])
+    local_waits["sg"].wait()
+    local_waits["su"].wait()
+    cur = c_all[...].reshape(total, width)
+    sh_part[:, :, :sh] = dot(cur, sg_v[...]).astype(BF).reshape(n_dp, share, sh)
+    sh_part[:, :, sh:] = dot(cur, su_v[...]).astype(BF).reshape(n_dp, share, sh)
+    for s in range(1, n_dp):
+        remote(sh_part.at[dp_dev(s)], sh_in.at[s], shp_s.at[s], shp_r.at[s], dp_dev(s), me_e)
     for q in range(PARTS):
-        routed_act(q)
+        routed_act(pairs - 1, q)
     term = sh_part[me_d].astype(F32)
     for s in range(1, n_dp):
         arrived(sh_in.at[s], shp_s.at[s], shp_r.at[s])
@@ -271,23 +290,32 @@
     sh_hid[me_d] = act(term, sh)
     for s in range(1, n_dp):
         remote(sh_hid.at[me_d], sh_hid.at[me_d], shh_s.at[s], shh_r.at[s], dp_dev(s), me_e)
-    for q in range(PARTS):
-        routed_down(q, q == 0)
-    for s in range(1, n_dp):
-        arrived(sh_hid.at[dp_src(s)], shh_s.at[s], shh_r.at[s])
-    local_waits["sd"].wait()
-    value = dot(sh_hid[...].reshape(total, sh), sd_v[...])
-    value = value + scale_col * dot(scatter, acc[...].astype(BF))
-    contrib[...] = value.astype(BF).reshape(n_e, tokens, width)
-    order = [*range(zs - 1, -1, -1)]
-    for s in order:
-        remote(contrib.at[2 * lax.rem(z + s, zs) + 1 - c], pair_in.at[s], pair_s.at[s], pair_r.at[s], me_d, partner)
-    for s in order:
-        arrived(pair_in.at[s], pair_s.at[s], pair_r.at[s])
-        both = contrib[z_dev(s)].astype(F32) + pair_in[s].astype(F32)
-        if s:
-            fin_out[s] = both.astype(BF)
-            remote(fin_out.at[s], fin_in.at[s], fin_s.at[s], fin_r.at[s], me_d, z_dev(s))
+
+    for a in range(pairs - 2, -1, -1):
+        for q in range(PARTS):
+            routed_act(a, q)
+    for a in range(pairs - 1, -1, -1):
+        routed_down(a)
+        if a == pairs - 1:
+            for s in range(1, n_dp):
+                arrived(sh_hid.at[dp_src(s)], shh_s.at[s], shh_r.at[s])
+            local_waits["sd"].wait()
+            shv[...] = dot(sh_hid[...].reshape(total, sh), sd_v[...]).reshape(n_e, tokens, width)
+        scatter, scale_col = combine[a]
+        value = scale_col * dot(scatter, acc[...].astype(BF))
+        value = value + shv[group_blocks(a)].reshape(held, width)
+        contrib[group_blocks(a)] = value.astype(BF).reshape(4, tokens, width)
+        for s in (2 * a + 1, 2 * a):
+            remote(contrib.at[z_src(s) + 1 - 2 * c], pair_in.at[s], pair_s.at[s], pair_r.at[s], me_d, partner)
+        for s in (2 * a + 1, 2 * a):
+            arrived(pair_in.at[s], pair_s.at[s], pair_r.at[s])
+            summed = contrib[z_src(s)].astype(F32) + pair_in[s].astype(F32)
+            if s:
+                fin_out[s] = summed.astype(BF)
+                remote(fin_out.at[s], fin_in.at[s], fin_s.at[s], fin_r.at[s], me_d, z_src(s))
+            else:
+                own_sum[...] = summed
+    both = own_sum[...]
     for s in range(1, zs):
         arrived(fin_in.at[s], fin_s.at[s], fin_r.at[s])
         both = both + fin_in[s].astype(F32)
@@ -301,11 +329,12 @@
     hidden = gate_weight.shape[2]
     top = expert_ids.shape[1]
     capacity = 3 * tokens * top // (2 * n_e)
-    rows = min(-(-capacity * n_e // 16) * 16, n_e * tokens)
+    rows = min(-(-capacity * 4 // 16) * 16, 4 * tokens)
     chunk = hidden // n_dp // PARTS
     count = PARTS * n_dp
     sh = hidden // n_e
     zs = n_e // 2
+    pairs = zs // 2
     total = n_e * tokens
     share = total // n_dp
     V = pltpu.VMEM
@@ -313,14 +342,14 @@
     scratch = [
         V((count, width, chunk), BF), V((count, width, chunk), BF), V((count, chunk, width), BF),
         V((width, sh), BF), V((width, sh), BF), V((sh, width), BF),
-        V((tokens, 128), F32), V((n_e, tokens, 128), F32), V((n_e, tokens, width), BF), V((n_e, tokens, width), BF),
-        V((rows, width), BF), V((count, rows, 2 * chunk), BF), V((count, rows, 2 * chunk), BF),
-        V((count, rows, chunk), BF), V((rows, width), F32),
-        V((n_dp, share, 2 * sh), BF), V((n_dp, share, 2 * sh), BF), V((n_dp, share, sh), BF),
+        V((-(-2 * top // 8) * 8, 128), F32), V((tokens, 128), F32), V((n_e, tokens, 128), F32), V((n_e, tokens, width), BF), V((n_e, tokens, width), BF),
+        V((pairs, rows, width), BF), V((pairs * count, rows, 2 * chunk), BF), V((pairs * count, rows, 2 * chunk), BF),
+        V((pairs * count, rows, chunk), BF), V((rows, width), F32), V((n_e, tokens, width), F32),
+        V((n_dp, share, 2 * sh), BF), V((n_dp, share, 2 * sh), BF), V((n_dp, share, sh), BF), V((tokens, width), F32),
         V((n_e, tokens, width), BF), V((zs, tokens, width), BF), V((zs, tokens, width), BF), V((zs, tokens, width), BF),
         S((count,)), S((count,)), S((count,)), S((3,)),
         *[S((zs,)) for _ in range(12)],
-        *[S((count,)) for _ in range(4)],
+        *[S((pairs * count,)) for _ in range(4)],
         *[S((n_dp,)) for _ in range(4)],
         *[S((zs,)) for _ in range(4)],
     ]
@@ -333,14 +362,14 @@
         out_specs=vm,
         scratch_shapes=scratch,
         compiler_params=pltpu.CompilerParams(collective_id=0, has_side_effects=True, vmem_limit_bytes=60 * 1024 * 1024),
-    )(shortcut_in, current_in, expert_ids, route_weight, gate_weight, up_weight, down_weight, shared_gate, shared_up, shared_down)
+    )(shortcut_in, current_in, expert_ids.T, route_weight.T, gate_weight, up_weight, down_weight, shared_gate, shared_up, shared_down)
 
 
 def body(n_dp, n_e, *arrays):
     tokens, width = arrays[0].shape
     experts, _, hidden = arrays[4].shape
     aligned = (
-        experts == 1 and n_e % 2 == 0 and n_e <= 128 and tokens % 16 == 0 and width % 128 == 0
+        experts == 1 and n_e % 4 == 0 and tokens <= 128 and n_e <= 128 and tokens % 16 == 0 and width % 128 == 0
         and hidden % (n_dp * PARTS * 128) == 0 and hidden % (n_e * 128) == 0
         and n_e * tokens % (n_dp * 16) == 0
     )

time: 46.5 us -> 42.4 us (0.912)
  local copies, waits for them, and re-layouts: 4.15 us -> 1.45 us
  Pallas kernels: 42.1 us -> 40.8 us
    unnamed x3 -> x1, local copies, waits for them, and re-layouts: 4.15 us -> 1.45 us
    pallas_call x1, Pallas kernels: 42.1 us -> 40.8 us  [fused(): pl.pallas_call(functools.partial(layer_kernel, n_dp, n_e, rows), out_shap...]
where the time goes in v2:
time: 42.4 us; the launch traced here: 42.2 us
  Pallas kernels  40.8 us (96%)
  local copies, waits for them, and re-layouts  1.45 us (3%)
    pallas_call x1, Pallas kernels, fused(): pl.pallas_call(functools.partial(layer_kernel, n_dp, n_e, rows), out_shap...  40.8 us
    unnamed x1, local copies, waits for them, and re-layouts  1.45 us

profile of v2, /device:TPU:0, one launch (start us, length us, event | category | flops | bytes accessed | tf_op | source)
XLA Modules:
  0.0 42.2 jit_solution(7038945323196627476)
XLA Ops:
  0.0 40.8 %shard_map.100 = bf16[16,1792]{1,0:T(8,128)(2,1)} custom-call(bf16[16,1792]{1,0:T(8,128)(2,1)} %x_ref.1, bf16[16,1792]{1,0:T(8,128)(2,1)} %cur_ref.1, s32[4,16]{1,0:T(4,128)} %bitcast.2, f32[4,16]{1,0:T(4,128)} %bitcast.3, bf16[1,1792,2048]{2,1,0:T(8,128)(2,1)} %gate_hbm.1, bf16[1,1792,2048]{2,1,0:T(8,128)(2,1)} %up_hbm.1, bf16[1,2048,1792]{2,1,0:T(8,128)(2,1)} %down_hbm.1, ...), custom_call_target="tpu_custom_call" | custom-call | tf_op jit(solution)/shard_map/pallas_call | solution.py:358
  40.8 1.4 %copy.12 = bf16[16,1792]{1,0:T(8,128)(2,1)} copy(bf16[16,1792]{1,0:T(8,128)(2,1)} %shard_map.100) | data formatting | bytes 114688
